TPU v7x, 256 devices: a 4x2x16 block of a 4x16x16 slice. The times are simulated.
256 devices in a mesh: win: 2 (over y), row: 128 (over x, z, core).
Axes of the slice: x: 4, y: 2, z: 16, core: 2. Of those that a mesh axis runs over, the one named last changes fastest.
The devices are a block of a 4x16x16 slice.
Arguments:
- spectra: bfloat16 [256, 2, 32768], P(('win', 'row')), parts along dimension 0, may hold values from -6 to 6
- pair_mask: int32 [128, 128], P('row'), may hold values from 0 to 1, as said below
- available: int32 [256], P('win'), parts along dimension 0, may hold values 0 or 1
Outputs:
- correlations: float32 [256, 128, 8192], P(('win', 'row')), parts along dimension 0
There are 2 independent parts, one for each index of `win`. A program takes and returns all parts, laid end to end along the dimension named above; an argument that names none is the same for every part. Nothing has to cross between parts.
Inputs may be any that keep to these rules, and one draw needn't show every extreme that they name: pair_mask[i, j] is 0 wherever j <= i.
All inputs are finite; a program needn't handle non-finite values.
Results may differ from a plain program's by a relative error of at most 0.0003.
Values may be sent and summed in bfloat16 or wider, within the bound.
No kernel may reach another device: no remote copies, remote signals or barrier semaphores. Data moves between devices by JAX's collectives and lax.ppermute only.
A program may use at most 128 MiB of HBM per device.

v0:
```python
import math
import jax
import jax.numpy as jnp
from jax import lax
from jax.sharding import PartitionSpec as P

LAGS = 8192
full_turn = 2.0 * math.pi


def build_tables(freq, lags):
    nfft = 2 * freq
    inner = min(128, lags // 2)
    column = nfft // inner
    depth = freq // column
    outer = lags // inner
    centre = lags // 2
    t_inner = jnp.arange(inner, dtype=jnp.int32)
    k_depth = jnp.arange(depth, dtype=jnp.int32)
    k_column = jnp.arange(column, dtype=jnp.int32)
    t_outer = jnp.arange(outer, dtype=jnp.int32)
    first = full_turn * (t_inner[:, None] * k_depth[None, :] % inner).astype(jnp.float32) / inner
    cos_first = jnp.cos(first)
    sin_first = jnp.sin(first)
    section_one = jnp.concatenate(
        [
            jnp.concatenate([cos_first, -sin_first], axis=1),
            jnp.concatenate([sin_first, cos_first], axis=1),
        ],
        axis=0,
    )
    twist = (
        full_turn
        * jnp.mod(k_column[None, :] * (t_inner[:, None] - centre), nfft).astype(jnp.float32)
        / nfft
    )
    second = (
        full_turn * (t_outer[:, None] * k_column[None, :] % column).astype(jnp.float32) / column
    )
    section_two = jnp.stack([jnp.cos(second), -jnp.sin(second)], axis=1)
    return (section_one, jnp.cos(twist), jnp.sin(twist), section_two)


def pair_block(own_wide, part, signs, tables):
    section_one, twist_cos, twist_sin, section_two = tables
    count = own_wide.shape[0]
    width = part.shape[0]
    freq = part.shape[2]
    inner = twist_cos.shape[0]
    column = twist_cos.shape[1]
    outer = section_two.shape[0]
    depth = freq // column
    other = part.astype(jnp.float32)
    real_part = (
        own_wide[:, None, 0, :] * other[None, :, 0, :]
        + own_wide[:, None, 1, :] * other[None, :, 1, :]
    )
    imag_part = (
        own_wide[:, None, 0, :] * other[None, :, 1, :]
        - own_wide[:, None, 1, :] * other[None, :, 0, :]
    ) * signs[:, :, None]
    cross = jnp.stack([real_part, imag_part], axis=2).reshape(count * width, 2 * depth, column)
    mixed = jnp.einsum("uv,pvk->puk", section_one, cross, precision=lax.Precision.HIGH)
    mixed = mixed.reshape(count * width, 2, inner, column)
    turned_real = mixed[:, 0] * twist_cos - mixed[:, 1] * twist_sin
    turned_imag = mixed[:, 0] * twist_sin + mixed[:, 1] * twist_cos
    turned = jnp.stack([turned_real, turned_imag], axis=1)
    summed = jnp.einsum("tck,pcuk->ptu", section_two, turned, precision=lax.Precision.HIGH)
    summed = summed.reshape(count, width, outer * inner)
    return (2.0 * summed - real_part[:, :, :1]) * (1.0 / math.sqrt(8.0 * freq))


def correlate(own, others, signs, tables):
    own_wide = own.astype(jnp.float32)
    count = own.shape[0]
    total = others.shape[0]
    width = math.gcd(total, max(1, 8 // count))
    groups = total // width
    pieces = others.reshape(groups, width, 2, others.shape[2])
    sign_pieces = jnp.transpose(signs.reshape(count, groups, width), (1, 0, 2))

    def one_group(item):
        return pair_block(own_wide, item[0], item[1], tables)

    results = lax.map(one_group, (pieces, sign_pieces))
    return jnp.transpose(results, (1, 0, 2, 3)).reshape(count, total, results.shape[3])


def per_device(spectra, pair_mask, available):
    count = spectra.shape[0]
    freq = spectra.shape[2]
    tables = build_tables(freq, LAGS)
    first_station = lax.axis_index("row") * count
    own_flags = lax.dynamic_slice_in_dim(available, first_station, count, 0).astype(jnp.float32)
    weight = (
        pair_mask.astype(jnp.float32) * own_flags[:, None] * available.astype(jnp.float32)[None, :]
    )
    piece = lax.all_gather(spectra, "row", axis=0, tiled=True)
    corr = correlate(spectra, piece, jnp.ones((count, piece.shape[0]), jnp.float32), tables)
    return corr * weight[:, :, None]


def solution(mesh):
    return jax.shard_map(
        per_device,
        mesh=mesh,
        in_specs=(P(("win", "row"), None, None), P("row", None), P("win")),
        out_specs=P(("win", "row"), None, None),
        check_vma=False,
    )
```

profile of v0, /device:TPU:33, one launch (start us, length us, event | category | flops | bytes accessed | tf_op | source)
XLA Modules:
  0.0 506.9 jit_solution(1056133077329128225)
XLA Ops:
  12.1 166.8 %all-gather.2.cloned.1.call-done = bf16[128,2,32768]{2,1,0:T(2,128)(2,1)} async-done(((bf16[1,2,32768]{2,1,0:T(2,128)(2,1)}), bf16[128,2,32768]{2,1,0:T(2,128)(2,1)}) %all-gather.2.cloned.1.call-update) | async-done | bytes 16777232 | tf_op jit(solution)/shard_map/all_gather | solution.py:98
  178.9 316.4 %while.13 = (s32[]{:T(128)}, f32[16,1,8,8192]{3,2,1,0:T(8,128)}, f32[1,2,32768]{2,1,0:T(2,128)S(1)}, bf16[16,8,2,32768]{3,2,1,0:T(2,128)(2,1)}, f32[256,128]{1,0...) while((s32[]{:T(128)}, f32[16,1,8,8192]{3,2,1,0:T(8,128)}, ...), condition=%wide.region_1.2_spmd.clone.clone.clone, body=%wide.region_0.1_spmd.clone.clone.clone.sunk | while | flops 1215889408 | bytes 57017112 | solution.py:85
  184.3 2.9 copy.24
  187.3 4.0 reshape.466
  192.9 2.2 fusion.71
  195.8 2.0 fusion.73
  204.1 2.9 copy.24
  207.0 4.0 reshape.466
  212.7 2.2 fusion.71
  215.6 2.0 fusion.73
  223.9 2.9 copy.24
  226.8 4.0 reshape.466
  232.5 2.2 fusion.71
  243.7 2.9 copy.24
  246.6 4.0 reshape.466
  252.3 2.2 fusion.71
  255.1 2.0 fusion.73
  263.4 2.9 copy.24
  266.4 4.0 reshape.466
  272.0 2.2 fusion.71
  274.9 2.0 fusion.73
  283.2 2.9 copy.24
  286.1 4.0 reshape.466
  291.8 2.2 fusion.71
  294.7 2.0 fusion.73
  303.0 2.9 copy.24
  305.9 4.0 reshape.466
  311.6 2.2 fusion.71
  314.5 2.0 fusion.73
  322.8 2.9 copy.24
  325.7 4.0 reshape.466
  331.4 2.2 fusion.71
  334.3 2.0 fusion.73
  342.5 2.9 copy.24
  345.5 4.0 reshape.466
  351.1 2.2 fusion.71
  354.0 2.0 fusion.73
  362.3 2.9 copy.24
  365.2 4.0 reshape.466
  370.9 2.2 fusion.71
  373.8 2.0 fusion.73
  382.1 2.9 copy.24
  385.0 4.0 reshape.466
  390.7 2.2 fusion.71
  393.6 2.0 fusion.73
  401.9 2.9 copy.24
  404.8 4.0 reshape.466
  410.5 2.2 fusion.71
  413.4 2.0 fusion.73
  421.7 2.9 copy.24
  424.6 4.0 reshape.466
  430.3 2.2 fusion.71
  433.2 2.0 fusion.73
  441.4 2.9 copy.24
  444.4 4.0 reshape.466
  450.0 2.2 fusion.71
  452.9 2.0 fusion.73
  461.2 2.9 copy.24
  464.1 4.0 reshape.466
  469.8 2.2 fusion.71
  481.0 2.9 copy.24
  483.9 4.0 reshape.466
  489.6 2.2 fusion.71
  495.3 4.7 bitcast_multiply_fusion.4
  (255 shorter events, 148.0 us)
Async XLA Ops:
  6.5 172.4 %all-gather.2.cloned.1.call-start = ((), (), s32[]{:S(2)}) async-start(), calls=%async_computation | async-start | bytes 16908288 | tf_op jit(solution)/shard_map/all_gather | solution.py:98
  191.3 1.6 copy-start
  211.1 1.6 copy-start
  230.8 1.6 copy-start
  250.6 1.6 copy-start
  270.4 1.6 copy-start
  290.2 1.6 copy-start
  310.0 1.6 copy-start
  329.7 1.6 copy-start
  349.5 1.6 copy-start
  369.3 1.6 copy-start
  389.1 1.6 copy-start
  408.8 1.6 copy-start
  428.6 1.6 copy-start
  448.4 1.6 copy-start
  468.2 1.6 copy-start
  488.0 1.6 copy-start
Sparse Core Ops, SparseCore 0:
  10.0 168.9 all-gather.1
where the time goes:
time: 508 us; the launch traced here: 507 us
  waiting for transfers between devices  168 us (33%)
  local copies, waits for them, and re-layouts  168 us (33%)
  other arithmetic  89.5 us (18%)
  matrix products  66.9 us (13%)
  between operations  14.1 us (3%)
    all_gather x1, waiting for transfers between devices, per_device(): piece = lax.all_gather(spectra, 'row', axis=0, tiled=True)  167 us
    reshape x16, local copies, waits for them, and re-layouts, pair_block(): jnp.stack([real_part, imag_part], axis=2)  64.5 us
    another operation x16, local copies, waits for them, and re-layouts, pair_block(): jnp.stack([real_part, imag_part], axis=2)  47 us
    dot_general x16, matrix products, pair_block(): jnp.einsum('uv,pvk->puk', section_one, cross, precision=lax.Precision.HIGH)  34.5 us
    dot_general x16, matrix products, pair_block(): jnp.einsum('tck,pcuk->ptu', section_two, turned, precision=lax.Precision....  32.4 us
    dynamic_slice x16, local copies, waits for them, and re-layouts, correlate(): results = lax.map(one_group, (pieces, sign_pieces))  31.2 us
    slice x16, other arithmetic, pair_block(): return (2.0 * summed - real_part[:, :, :1]) * (1.0 / math.sqrt(8.0 * freq))  24 us
    slice x32, local copies, waits for them, and re-layouts, pair_block(): return (2.0 * summed - real_part[:, :, :1]) * (1.0 / math.sqrt(8.0 * freq))  17.6 us
  transfers between devices with their start and end apart: 1, of which 1 were waited for; matrix products, arithmetic and copies ran while one was open for 1% of the time, Pallas kernels for 0%

commit v1 on v0

--- a/solution.py
+++ b/solution.py
@@ -6,6 +6,13 @@
 
 LAGS = 8192
 full_turn = 2.0 * math.pi
+
+
+def knots_launch(along_axis, arr):
+    opened = jnp.concatenate(
+        lax.all_to_all(jnp.stack([arr] * lax.psum(1, along_axis)), along_axis, 0, 0), axis=0
+    )
+    return opened
 
 
 def build_tables(freq, lags):
@@ -95,7 +102,7 @@
     weight = (
         pair_mask.astype(jnp.float32) * own_flags[:, None] * available.astype(jnp.float32)[None, :]
     )
-    piece = lax.all_gather(spectra, "row", axis=0, tiled=True)
+    piece = knots_launch("row", spectra)
     corr = correlate(spectra, piece, jnp.ones((count, piece.shape[0]), jnp.float32), tables)
     return corr * weight[:, :, None]
 

time: 508 us -> 1110 us (2.19)
  waiting for transfers between devices: 168 us -> 719 us
  starting transfers between devices: 0.01 us -> 31.2 us
  matrix products: 66.9 us -> 92.3 us
  between operations: 14.1 us -> 0.77 us
    all_to_all x0 -> x1, waiting for transfers between devices: none -> 719 us  [knots_launch(): lax.all_to_all(jnp.stack([arr] * lax.psum(1, along_axis)), along_axis, 0, 0)]
    all_gather x1 -> x0, waiting for transfers between devices: 167 us -> none  [per_device(): piece = lax.all_gather(spectra, 'row', axis=0, tiled=True)]
    all_to_all x0 -> x1, starting transfers between devices: none -> 31.2 us  [knots_launch(): lax.all_to_all(jnp.stack([arr] * lax.psum(1, along_axis)), along_axis, 0, 0)]
    dot_general x16, matrix products: 34.5 us -> 59.9 us  [pair_block(): jnp.einsum('uv,pvk->puk', section_one, cross, precision=lax.Precision.HIGH)]
    another operation x0 -> x1, local copies, waits for them, and re-layouts: none -> 11.2 us  [knots_launch(): jnp.stack([arr] * lax.psum(1, along_axis))]
  transfers between devices with their start and end apart: 1 -> 1, of which waited for: 1 -> 1; matrix products, arithmetic and copies ran while one was open for 1% -> 0% of each run, Pallas kernels for 0% -> 0%
where the time goes in v1:
time: 1110 us
  waiting for transfers between devices  719 us (65%)
  local copies, waits for them, and re-layouts  178 us (16%)
  matrix products  92.3 us (8%)
  other arithmetic  84.3 us (8%)
  starting transfers between devices  31.2 us (3%)
    all_to_all x1, waiting for transfers between devices, knots_launch(): lax.all_to_all(jnp.stack([arr] * lax.psum(1, along_axis)), along_axis, 0, 0)  719 us
    reshape x16, local copies, waits for them, and re-layouts, pair_block(): jnp.stack([real_part, imag_part], axis=2)  64.9 us
    dot_general x16, matrix products, pair_block(): jnp.einsum('uv,pvk->puk', section_one, cross, precision=lax.Precision.HIGH)  59.9 us
    another operation x16, local copies, waits for them, and re-layouts, pair_block(): jnp.stack([real_part, imag_part], axis=2)  47 us
    dot_general x16, matrix products, pair_block(): jnp.einsum('tck,pcuk->ptu', section_two, turned, precision=lax.Precision....  32.4 us
    all_to_all x1, starting transfers between devices, knots_launch(): lax.all_to_all(jnp.stack([arr] * lax.psum(1, along_axis)), along_axis, 0, 0)  31.2 us
    dynamic_slice x16, local copies, waits for them, and re-layouts, correlate(): results = lax.map(one_group, (pieces, sign_pieces))  31.1 us
  transfers between devices with their start and end apart: 1, of which 1 were waited for; matrix products, arithmetic and copies ran while one was open for 0% of the time, Pallas kernels for 0%

profile of v1, /device:TPU:33, one launch (start us, length us, event | category | flops | bytes accessed | tf_op | source)
XLA Modules:
  0.0 1107.1 jit_solution(1498292546320732834)
XLA Ops:
  0.0 11.2 %stack.8 = bf16[128,1,2,32768]{3,2,1,0:T(2,128)(2,1)} broadcast(bf16[2,32768]{1,0:T(2,128)(2,1)} %bitcast.84), dimensions={2,3} | broadcast | bytes 16908288 | tf_op jit(solution)/shard_map/stack | solution.py:13
  11.3 31.2 %all-to-all-start = ((bf16[128,1,2,32768]{3,2,1,0:T(2,128)(2,1)}), bf16[128,1,2,32768]{3,2,1,0:T(2,128)(2,1)}, u32[]{:S(2)}, u32[]{:S(2)}) async-start(bf16[128,1,2,32768]{3,2,1,0:T(2,128)(2,1)} %stack.8), calls=%async_computation | async-start | bytes 33554432 | tf_op jit(solution)/shard_map/all_to_all | solution.py:13
  45.1 718.9 %all-to-all-done = bf16[128,1,2,32768]{3,2,1,0:T(2,128)(2,1)} async-done(((bf16[128,1,2,32768]{3,2,1,0:T(2,128)(2,1)}), bf16[128,1,2,32768]{3,2,1,0:T(2,128)(2,1)}, u32[]{:S(2)}, u32[]{:S(2)}) %all-to-all-start) | async-done | bytes 16777248 | tf_op jit(solution)/shard_map/all_to_all | solution.py:13
  764.0 338.5 %while.13 = (s32[]{:T(128)}, f32[16,1,8,8192]{3,2,1,0:T(8,128)}, f32[1,2,32768]{2,1,0:T(2,128)S(1)}, bf16[16,8,2,32768]{3,2,1,0:T(2,128)(2,1)}, f32[256,128]{1,0...) while((s32[]{:T(128)}, f32[16,1,8,8192]{3,2,1,0:T(8,128)}, ...), condition=%wide.region_1.2_spmd.clone.clone.clone, body=%wide.region_0.1_spmd.clone.clone.clone.sunk | while | flops 1215889408 | bytes 48628976 | solution.py:92
  767.2 2.9 copy.23
  770.1 4.1 reshape.465
  774.2 3.7 fusion.71
  779.7 2.0 fusion.73
  788.3 2.9 copy.23
  791.3 4.1 reshape.465
  795.3 3.7 fusion.71
  800.9 2.0 fusion.73
  809.5 2.9 copy.23
  812.4 4.1 reshape.465
  816.5 3.7 fusion.71
  822.0 2.0 fusion.73
  830.7 2.9 copy.23
  833.6 4.1 reshape.465
  837.7 3.7 fusion.71
  851.8 2.9 copy.23
  854.8 4.1 reshape.465
  858.8 3.7 fusion.71
  864.3 2.0 fusion.73
  873.0 2.9 copy.23
  875.9 4.1 reshape.465
  880.0 3.7 fusion.71
  894.1 2.9 copy.23
  897.1 4.1 reshape.465
  901.1 3.7 fusion.71
  906.6 2.0 fusion.73
  915.3 2.9 copy.23
  918.2 4.1 reshape.465
  922.3 3.7 fusion.71
  936.4 2.9 copy.23
  939.4 4.1 reshape.465
  943.4 3.7 fusion.71
  948.9 2.0 fusion.73
  957.6 2.9 copy.23
  960.5 4.1 reshape.465
  964.6 3.7 fusion.71
  978.7 2.9 copy.23
  981.7 4.1 reshape.465
  985.7 3.7 fusion.71
  999.9 2.9 copy.23
  1002.8 4.1 reshape.465
  1006.9 3.7 fusion.71
  1012.4 2.0 fusion.73
  1021.0 2.9 copy.23
  1023.9 4.1 reshape.465
  1028.0 3.7 fusion.71
  1033.5 2.0 fusion.73
  1042.2 2.9 copy.23
  1045.1 4.1 reshape.465
  1049.2 3.7 fusion.71
  1054.7 2.0 fusion.73
  1063.3 2.9 copy.23
  1066.3 4.1 reshape.465
  1070.3 3.7 fusion.71
  1075.8 2.0 fusion.73
  1084.5 2.9 copy.23
  1087.4 4.1 reshape.465
  1091.5 3.7 fusion.71
  1097.0 2.0 fusion.73
  1102.5 4.7 bitcast_multiply_fusion.4
  (229 shorter events, 145.1 us)
Async XLA Ops:
  11.2 31.3 %copy-start = (bf16[1,2,32768]{2,1,0:T(2,128)(2,1)S(1)}, bf16[1,2,32768]{2,1,0:T(2,128)(2,1)}, u32[]{:S(2)}) copy-start(bf16[1,2,32768]{2,1,0:T(2,128)(2,1)} %param.5) | copy-start | bytes 393220
  11.2 31.4 %copy-start.1 = (s32[128]{0:T(128)S(1)}, s32[128]{0:T(128)}, u32[]{:S(2)}) copy-start(s32[128]{0:T(128)} %param.7) | copy-start | bytes 1540
  11.3 33.9 %copy-start.2 = (s32[1,128]{1,0:T(1,128)S(1)}, s32[1,128]{1,0:T(1,128)}, u32[]{:S(2)}) copy-start(s32[1,128]{1,0:T(1,128)} %param.6) | copy-start | bytes 1540
  11.3 752.8 %all-to-all-start = ((bf16[128,1,2,32768]{3,2,1,0:T(2,128)(2,1)}), bf16[128,1,2,32768]{3,2,1,0:T(2,128)(2,1)}, u32[]{:S(2)}, u32[]{:S(2)}) async-start(bf16[128,1,2,32768]{3,2,1,0:T(2,128)(2,1)} %stack.8), calls=%async_computation | async-start | bytes 33554432 | tf_op jit(solution)/shard_map/all_to_all | solution.py:13
